TPU v7x, 32 devices: a whole 2x2x4 slice. The times are simulated.
32 devices in a mesh: replica: 8 (over z, core), ctx: 4 (over y, x).
Axes of the slice: x: 2, y: 2, z: 4, core: 2. Of those that a mesh axis runs over, the one named last changes fastest.
Arguments:
- queries: bfloat16 [32, 128, 3584], P('replica', 'ctx'), may hold values from -128 to 128
- key_cache: bfloat16 [4096, 512], P('ctx'), may hold values from -6 to 6
- value_cache: bfloat16 [4096, 512], P('ctx'), may hold values from -6 to 6
- key_scale: float32 [32, 4], P('ctx'), may hold values from 0.7 to 1.4
- value_scale: float32 [32, 4], P('ctx'), may hold values from 0.5 to 2
- pattern: int32 [28, 32, 32], replicated, may hold values from 0 to 31
- target: int32 [32], replicated, may hold values from 0 to 7, as said below
Outputs:
- landed: bfloat16 [32, 128, 3584], P('replica', 'ctx')
Inputs may be any that keep to these rules, and one draw needn't show every extreme that they name: `target`: query block j belongs to group j // 4. The blocks of one group go to distinct groups, and every group receives exactly 4 blocks.
All inputs are finite; a program needn't handle non-finite values.
Results may differ from a plain program's by a relative error of at most 0.018.
Values may be sent and summed in bfloat16 or wider, within the bound.
No kernel may reach another device: no remote copies, remote signals or barrier semaphores. Data moves between devices by JAX's collectives and lax.ppermute only.
A program may use at most 64 MiB of HBM per device.

v0:
```python
import math
import jax
import jax.numpy as jnp
from jax import lax
from jax.sharding import PartitionSpec as P


def arrivals(target, group_index, group_count, per_group):
    block_grid = target.reshape(group_count, per_group)
    hit_table = (block_grid == group_index).astype(jnp.int32)
    coming = jnp.sum(hit_table, axis=1)
    arrival_slot = jnp.cumsum(coming) - 1
    places = jnp.arange(per_group, dtype=jnp.int32)
    matched = (coming[None, :] > 0) & (arrival_slot[None, :] == places[:, None])
    anchor = jnp.arange(group_count, dtype=jnp.int32) * per_group + jnp.sum(
        hit_table * places[None, :], axis=1
    )
    arriving = jnp.sum(jnp.where(matched, anchor[None, :], 0), axis=1)
    return (matched.astype(jnp.bfloat16), arriving)


def relocate(blocks, target, group_index, group_count, per_group, picker):
    own_targets = lax.dynamic_slice_in_dim(target, group_index * per_group, per_group)
    outgoing = (own_targets[None, :] == jnp.arange(group_count, dtype=jnp.int32)[:, None]).astype(
        jnp.bfloat16
    )
    packed = jnp.einsum("dk,kxh->dxh", outgoing, blocks, preferred_element_type=jnp.float32).astype(
        jnp.bfloat16
    )
    received = lax.all_to_all(packed, "replica", split_axis=0, concat_axis=0, tiled=True)
    return jnp.einsum("sr,rxh->sxh", picker, received, preferred_element_type=jnp.float32).astype(
        jnp.bfloat16
    )


def collect(blocks):
    return lax.all_gather(blocks, "ctx", axis=1, tiled=True)


def attend(
    whole,
    block_list,
    key_cache,
    value_cache,
    key_scale,
    value_scale,
    pattern,
    shard_index,
    kv_blocks,
):
    block_count, block_rows, row_width = whole.shape
    kv_heads = key_scale.shape[1]
    head_size = key_cache.shape[1] // kv_heads
    head_count = row_width // head_size
    group_size = head_count // kv_heads
    local_blocks = key_cache.shape[0] // block_rows
    first_block = kv_blocks - pattern.shape[1]
    query = whole.reshape(block_count, block_rows, kv_heads, group_size, head_size)
    keys = key_cache.reshape(local_blocks, block_rows, kv_heads, head_size)
    values = value_cache.reshape(local_blocks, block_rows, kv_heads, head_size)
    listed = jnp.take(pattern, block_list, axis=1).reshape(
        kv_heads, group_size, block_count, pattern.shape[2]
    )
    diagonal = first_block + block_list
    row_ids = jnp.arange(block_rows, dtype=jnp.int32)
    block_ids = shard_index * local_blocks + jnp.arange(local_blocks, dtype=jnp.int32)
    key_pos = block_ids[:, None] * block_rows + row_ids[None, :]
    inv_root = 1.0 / math.sqrt(head_size)

    def one_item(item):
        block_slot = item // kv_heads
        head = item % kv_heads
        query_tile = lax.dynamic_index_in_dim(
            lax.dynamic_index_in_dim(query, block_slot, 0, keepdims=False), head, 1, keepdims=False
        )
        key_head = lax.dynamic_index_in_dim(keys, head, 2, keepdims=False)
        value_head = lax.dynamic_index_in_dim(values, head, 2, keepdims=False)
        heads_listed = lax.dynamic_index_in_dim(
            lax.dynamic_index_in_dim(listed, head, 0, keepdims=False), block_slot, 1, keepdims=False
        )
        diag = lax.dynamic_index_in_dim(diagonal, block_slot, 0, keepdims=False)
        chosen = (
            jnp.any(heads_listed[:, :, None] == block_ids[None, None, :], axis=1)
            | (block_ids == diag)[None, :]
        )
        query_pos = diag * block_rows + row_ids
        causal = key_pos[None, :, :] <= query_pos[:, None, None]
        allowed = chosen[:, None, :, None] & causal[None]
        key_factor = lax.dynamic_index_in_dim(key_scale, head, 1, keepdims=False) * inv_root
        value_factor = lax.dynamic_index_in_dim(value_scale, head, 1, keepdims=False)
        product = jnp.einsum(
            "rkd,btd->krbt", query_tile, key_head, preferred_element_type=jnp.float32
        )
        scores = product * key_factor[None, None, :, None]
        local_top = jnp.max(jnp.where(allowed, scores, -jnp.inf), axis=(2, 3))
        expo = jnp.where(allowed, jnp.exp(scores - local_top[:, :, None, None]), 0.0)
        weight = (expo * value_factor[None, None, :, None]).astype(jnp.bfloat16)
        numer = jnp.einsum("krbt,btd->rkd", weight, value_head, preferred_element_type=jnp.float32)
        denom = jnp.transpose(jnp.sum(expo, axis=(2, 3)))
        return (numer, denom, jnp.transpose(local_top))

    numer_all, denom_all, top_all = lax.map(
        one_item, jnp.arange(block_count * kv_heads, dtype=jnp.int32)
    )
    numer_all = numer_all.reshape(block_count, kv_heads, block_rows, group_size, head_size)
    denom_all = denom_all.reshape(block_count, kv_heads, block_rows, group_size)
    local_top = top_all.reshape(block_count, kv_heads, block_rows, group_size)
    top_score = lax.pmax(local_top.astype(jnp.bfloat16), "ctx").astype(local_top.dtype)
    rescale = jnp.exp(local_top - top_score)
    numer_scaled = jnp.transpose(numer_all * rescale[..., None], (0, 2, 1, 3, 4)).reshape(
        block_count, block_rows, row_width
    )
    denom_scaled = jnp.transpose(denom_all * rescale, (0, 2, 1, 3)).reshape(
        block_count, block_rows, head_count
    )
    numer_sum, denom_sum = (
        lax.psum_scatter(
            numer_scaled.astype(jnp.bfloat16), "ctx", scatter_dimension=1, tiled=True
        ).astype(jnp.float32),
        lax.psum_scatter(
            denom_scaled.astype(jnp.bfloat16), "ctx", scatter_dimension=1, tiled=True
        ).astype(jnp.float32),
    )
    own_rows = numer_sum.shape[1]
    attended = (
        numer_sum.reshape(block_count, own_rows, head_count, head_size) / denom_sum[..., None]
    )
    return attended.reshape(block_count, own_rows, row_width).astype(jnp.bfloat16)


def per_device(queries, key_cache, value_cache, key_scale, value_scale, pattern, target):
    group_count = lax.axis_size("replica")
    shard_count = lax.axis_size("ctx")
    group_index = lax.axis_index("replica")
    shard_index = lax.axis_index("ctx")
    per_group = queries.shape[0]
    block_rows = queries.shape[1] * shard_count
    kv_blocks = key_cache.shape[0] // block_rows * shard_count
    picker, arriving = arrivals(target, group_index, group_count, per_group)
    moved = relocate(queries, target, group_index, group_count, per_group, picker)
    whole = collect(moved)
    return attend(
        whole,
        arriving,
        key_cache,
        value_cache,
        key_scale,
        value_scale,
        pattern,
        shard_index,
        kv_blocks,
    )


def solution(mesh):
    return jax.shard_map(
        per_device,
        mesh=mesh,
        in_specs=(
            P("replica", "ctx", None),
            P("ctx", None),
            P("ctx", None),
            P("ctx", None),
            P("ctx", None),
            P(),
            P(),
        ),
        out_specs=P("replica", "ctx", None),
        check_vma=False,
    )
```

profile of v0, /device:TPU:0, one launch (start us, length us, event | category | flops | bytes accessed | tf_op | source)
XLA Modules:
  0.0 480.7 jit_solution(8024060534990406194)
XLA Ops:
  8.8 1.8 copy.52
  10.5 6.4 %all-to-all-start = ((bf16[8,32,3584]{2,1,0:T(8,128)(2,1)}), bf16[8,32,3584]{2,1,0:T(8,128)(2,1)S(1)}, u32[]{:S(2)}, u32[]{:S(2)}) async-start(bf16[8,32,3584]{2,1,0:T(8,128)(2,1)} %copy.52), calls=%async_computation | async-start | bytes 3670016 | tf_op jit(solution)/shard_map/all_to_all | solution.py:30
  17.4 42.9 %all-to-all-done = bf16[8,32,3584]{2,1,0:T(8,128)(2,1)S(1)} async-done(((bf16[8,32,3584]{2,1,0:T(8,128)(2,1)}), bf16[8,32,3584]{2,1,0:T(8,128)(2,1)S(1)}, u32[]{:S(2)}, u32[]{:S(2)}) %all-to-all-start) | async-done | bytes 1835040 | tf_op jit(solution)/shard_map/all_to_all | solution.py:30
  60.3 2.9 convolution_convert_fusion.1
  67.8 42.8 %all-gather.2.cloned.1.call-done = bf16[4,128,3584]{2,0,1:T(4,128)(2,1)} async-done(((bf16[4,32,3584]{2,0,1:T(4,128)(2,1)}), bf16[4,128,3584]{2,0,1:T(4,128)(2,1)}) %all-gather.2.cloned.1.call-update) | async-done | bytes 3670032 | tf_op jit(solution)/shard_map/all_gather | solution.py:37
  110.6 7.2 %copy.54 = bf16[4,128,3584]{1,2,0:T(8,128)(2,1)} copy(bf16[4,128,3584]{2,0,1:T(4,128)(2,1)} %all-gather.2.cloned.1.call-done) | data formatting | bytes 7340032 | tf_op jit(solution)/shard_map/all_gather | solution.py:37
  117.8 209.7 %while.18 = (s32[]{:T(128)}, f32[16,128,7,128]{1,3,2,0:T(8,128)}, f32[16,128,7]{1,2,0:T(8,128)S(1)}, f32[16,128,7]{1,2,0:T(8,128)S(1)}, s32[16]{0:T(128)S(1)}, /...) while((s32[]{:T(128)}, f32[16,128,7,128]{1,3,2,0:T(8,128)}, ...), condition=%wide.region_8.9_spmd.clone, body=%wide.region_4.8_spmd.clone.sunk | while | flops 483658688 | bytes 12792716 | solution.py:102
  124.3 1.7 fusion.45
  127.8 3.1 fusion.47
  137.4 1.7 fusion.45
  140.9 3.1 fusion.47
  150.5 1.7 fusion.45
  154.1 3.1 fusion.47
  163.6 1.7 fusion.45
  167.2 3.1 fusion.47
  176.8 1.7 fusion.45
  180.3 3.1 fusion.47
  189.9 1.7 fusion.45
  193.4 3.1 fusion.47
  203.0 1.7 fusion.45
  206.5 3.1 fusion.47
  216.1 1.7 fusion.45
  219.6 3.0 fusion.47
  229.2 1.7 fusion.45
  232.7 3.1 fusion.47
  242.3 1.7 fusion.45
  245.8 3.1 fusion.47
  255.4 1.7 fusion.45
  258.9 3.0 fusion.47
  268.5 1.7 fusion.45
  272.0 3.1 fusion.47
  281.6 1.7 fusion.45
  285.1 3.1 fusion.47
  294.7 1.7 fusion.45
  298.2 3.0 fusion.47
  307.8 1.7 fusion.45
  311.3 3.1 fusion.47
  320.9 1.7 fusion.45
  324.4 3.1 fusion.47
  327.5 15.4 %pmax.7 = bf16[4,4,128,7]{2,0,3,1:T(4,128)(2,1)S(1)} all-reduce(bf16[4,4,128,7]{2,0,3,1:T(4,128)(2,1)S(1)} %copy.87), channel_id=1, replica_groups=mesh['replica'=8,'ctx'=4] {'ctx'}, use_global_device_ids=true, to_apply=%region_9.10 | all-reduce | flops 14336 | bytes 57344 | tf_op jit(solution)/shard_map/pmax | solution.py:108
  343.1 1.5 copy.73
  344.6 2.3 reshape.165
  347.0 6.2 %multiply_convert_fusion.6 = bf16[4,4,128,7,128]{2,4,3,1,0:T(8,128)(2,1)} fusion(f32[4,4,128,7,128]{2,4,3,1,0:T(8,128)} %bitcast.9, f32[4,4,128,7]{2,3,1,0:T(8,128)S(1)} %copy.60), kind=kLoop, calls=%fused_computation.39 | loop fusion | flops 3670016 | bytes 11067392 | tf_op jit(solution)/shard_map/convert_element_type | solution.py:118
  353.3 7.3 %copy.61 = bf16[4,128,3584]{2,0,1:T(4,128)(2,1)} copy(bf16[4,128,3584]{1,2,0:T(8,128)(2,1)} %bitcast.121) | data formatting | bytes 7340032 | tf_op jit(solution)/shard_map/convert_element_type | solution.py:118
  362.6 8.6 %reduce-scatter.4.cloned.1.call-done = bf16[32,112]{1,0:T(8,128)(2,1)} async-done(((bf16[128,112]{1,0:T(8,128)(2,1)}), bf16[32,112]{1,0:T(8,128)(2,1)}) %reduce-scatter.4.cloned.1.call-update) | async-done | bytes 7184
  373.4 1.6 div.20
  375.1 94.9 %all-reduce.3.cloned.1.call-done = bf16[4,128,3584]{2,0,1:T(4,128)(2,1)} async-done(((bf16[4,128,3584]{2,0,1:T(4,128)(2,1)}), bf16[4,128,3584]{2,0,1:T(4,128)(2,1)}) %all-reduce.3.cloned.1.call-update) | async-done | bytes 3670032
  471.4 2.7 divide_convert_fusion
  (291 shorter events, 92.0 us)
Async XLA Ops:
  6.5 1.2 copy-start
  8.7 8.2 %copy-start.4 = (s32[32]{0:T(128)S(1)}, s32[32]{0:T(128)}, u32[]{:S(2)}) copy-start(s32[32]{0:T(128)} %param.15) | copy-start | bytes 388
  10.5 49.8 %all-to-all-start = ((bf16[8,32,3584]{2,1,0:T(8,128)(2,1)}), bf16[8,32,3584]{2,1,0:T(8,128)(2,1)S(1)}, u32[]{:S(2)}, u32[]{:S(2)}) async-start(bf16[8,32,3584]{2,1,0:T(8,128)(2,1)} %copy.52), calls=%async_computation | async-start | bytes 3670016 | tf_op jit(solution)/shard_map/all_to_all | solution.py:30
  16.9 93.7 %all-gather.2.cloned.1.call-start = ((), (), s32[]{:S(2)}) async-start(), calls=%async_computation.2 | async-start | bytes 4587520 | tf_op jit(solution)/shard_map/all_gather | solution.py:37
  63.2 3.0 copy-start.1
  63.3 307.9 %reduce-scatter.4.cloned.1.call-start = ((), (), s32[]{:S(2)}) async-start(), calls=%async_computation.3 | async-start | bytes 40960
  64.8 2.1 copy-start.2
  67.7 50.1 %copy-start.3 = (f32[16,128,7]{1,2,0:T(8,128)S(1)}, f32[16,128,7]{1,2,0:T(8,128)}, u32[]{:S(2)}) copy-start(f32[16,128,7]{1,2,0:T(8,128)} %custom-call.3) | copy-start | bytes 172036
  347.0 123.0 %all-reduce.3.cloned.1.call-start = ((), (), s32[]{:S(2)}) async-start(), calls=%async_computation.4 | async-start | bytes 7340032
  360.6 0.7 copy-start.5
Sparse Core Ops, SparseCore 0:
  63.4 47.1 all-gather.1
  347.1 23.9 reduce-scatter.3
  374.2 95.6 all-reduce.2
where the time goes:
time: 484 us; the launch traced here: 481 us
  waiting for transfers between devices  189 us (39%)
  matrix products  80.3 us (17%)
  local copies, waits for them, and re-layouts  63.9 us (13%)
  other arithmetic  57.7 us (12%)
  loops' own time  53.7 us (11%)
  blocking collectives  15.4 us (3%)
  between operations  14 us (3%)
  starting transfers between devices  6.47 us (1%)
    unnamed x5, waiting for transfers between devices  104 us
    another operation x1, loops' own time, attend(): lax.map(one_item, jnp.arange(block_count * kv_heads, dtype=jnp.int32))  53.7 us
    dot_general x16, matrix products, one_item(): jnp.einsum('krbt,btd->rkd', weight, value_head, preferred_element_type=jn...  49 us
    all_to_all x1, waiting for transfers between devices, relocate(): lax.all_to_all(packed, 'replica', split_axis=0, concat_axis=0, tiled=True)  42.9 us
    all_gather x1, waiting for transfers between devices, collect(): return lax.all_gather(blocks, 'ctx', axis=1, tiled=True)  42.8 us
    dot_general x16, matrix products, one_item(): jnp.einsum('rkd,btd->krbt', query_tile, key_head, preferred_element_type=...  27.4 us
    reduce_sum x16, other arithmetic, one_item(): denom = jnp.transpose(jnp.sum(expo, axis=(2, 3)))  17.3 us
    pmax x1, blocking collectives, attend(): lax.pmax(local_top.astype(jnp.bfloat16), 'ctx').astype(local_top.dtype)  15.4 us
  transfers between devices with their start and end apart: 4, of which 4 were waited for; matrix products, arithmetic and copies ran while one was open for 5% of the time, Pallas kernels for 0%

commit v1 on v0

--- a/solution.py
+++ b/solution.py
@@ -3,6 +3,28 @@
 import jax.numpy as jnp
 from jax import lax
 from jax.sharding import PartitionSpec as P
+
+
+def laid_out(blocks, dim):
+    shape = list(blocks.shape[1:])
+    shape[dim] *= blocks.shape[0]
+    return jnp.moveaxis(blocks, 0, dim).reshape(shape)
+
+
+def collected_by_bits(x, axis):
+    length = lax.axis_size(axis)
+    tiles = x[None]
+    for level in range(length.bit_length() - 1):
+        bit = 1 << level
+        received = lax.ppermute(tiles, axis, [(i, i ^ bit) for i in range(length)])
+        both = jnp.stack([tiles, received])
+        upper = lax.axis_index(axis) >> level & 1
+        tiles = jnp.where(upper == 0, both, both[::-1]).reshape(-1, *x.shape)
+    return tiles
+
+
+def collect_2(x, axis, dim):
+    return laid_out(collected_by_bits(x, axis), dim)
 
 
 def arrivals(target, group_index, group_count, per_group):
@@ -34,7 +56,7 @@
 
 
 def collect(blocks):
-    return lax.all_gather(blocks, "ctx", axis=1, tiled=True)
+    return collect_2(blocks, "ctx", 1)
 
 
 def attend(

time: 484 us -> 525 us (1.085)
  local copies, waits for them, and re-layouts: 63.9 us -> 81.5 us
  other arithmetic: 57.7 us -> 67.6 us
    ppermute x0 -> x2, waiting for transfers between devices: none -> 49.5 us  [collected_by_bits(): received = lax.ppermute(tiles, axis, [(i, i ^ bit) for i in range(length)])]
    all_gather x1 -> x0, waiting for transfers between devices: 42.8 us -> none  [collect(): return lax.all_gather(blocks, 'ctx', axis=1, tiled=True)]
    unnamed x20 -> x19, local copies, waits for them, and re-layouts: 10.3 us -> 19.2 us
    another operation x0 -> x1, local copies, waits for them, and re-layouts: none -> 8.28 us  [attend(): whole.reshape(block_count, block_rows, kv_heads, group_size, head_size)]
    another operation x3 -> x6, other arithmetic: 0.19 us -> 8 us  [the longest x3 7.82 us: collected_by_bits(): both = jnp.stack([tiles, received])]
    all_gather x1 -> x0, local copies, waits for them, and re-layouts: 7.22 us -> none  [collect(): return lax.all_gather(blocks, 'ctx', axis=1, tiled=True)]
    unnamed x5 -> x4, waiting for transfers between devices: 104 us -> 102 us
  transfers between devices with their start and end apart: 4 -> 5, of which waited for: 4 -> 5; matrix products, arithmetic and copies ran while one was open for 5% -> 6% of each run, Pallas kernels for 0% -> 0%
where the time goes in v1:
time: 525 us; the launch traced here: 521 us
  waiting for transfers between devices  194 us (37%)
  local copies, waits for them, and re-layouts  81.5 us (16%)
  matrix products  80.9 us (15%)
  other arithmetic  67.6 us (13%)
  loops' own time  57 us (11%)
  blocking collectives  16.3 us (3%)
  between operations  14.3 us (3%)
  starting transfers between devices  9.51 us (2%)
    unnamed x4, waiting for transfers between devices  102 us
    another operation x1, loops' own time, attend(): lax.map(one_item, jnp.arange(block_count * kv_heads, dtype=jnp.int32))  57 us
    ppermute x2, waiting for transfers between devices, collected_by_bits(): received = lax.ppermute(tiles, axis, [(i, i ^ bit) for i in range(length)])  49.5 us
    dot_general x16, matrix products, one_item(): jnp.einsum('krbt,btd->rkd', weight, value_head, preferred_element_type=jn...  49 us
    all_to_all x1, waiting for transfers between devices, relocate(): lax.all_to_all(packed, 'replica', split_axis=0, concat_axis=0, tiled=True)  42.9 us
    dot_general x16, matrix products, one_item(): jnp.einsum('rkd,btd->krbt', query_tile, key_head, preferred_element_type=...  28.9 us
    unnamed x19, local copies, waits for them, and re-layouts  19.2 us
    reduce_sum x16, other arithmetic, one_item(): denom = jnp.transpose(jnp.sum(expo, axis=(2, 3)))  17.3 us
  transfers between devices with their start and end apart: 5, of which 5 were waited for; matrix products, arithmetic and copies ran while one was open for 6% of the time, Pallas kernels for 0%

profile of v1, /device:TPU:0, one launch (start us, length us, event | category | flops | bytes accessed | tf_op | source)
XLA Modules:
  0.0 521.1 jit_solution(16512479463608945019)
XLA Ops:
  10.5 6.4 %all-to-all-start = ((bf16[8,32,3584]{2,1,0:T(8,128)(2,1)}), bf16[8,32,3584]{2,1,0:T(8,128)(2,1)S(1)}, u32[]{:S(2)}, u32[]{:S(2)}) async-start(bf16[8,32,3584]{2,1,0:T(8,128)(2,1)} %copy.51), calls=%async_computation | async-start | bytes 3670016 | tf_op jit(solution)/shard_map/all_to_all | solution.py:52
  17.4 42.9 %all-to-all-done = bf16[8,32,3584]{2,1,0:T(8,128)(2,1)S(1)} async-done(((bf16[8,32,3584]{2,1,0:T(8,128)(2,1)}), bf16[8,32,3584]{2,1,0:T(8,128)(2,1)S(1)}, u32[]{:S(2)}, u32[]{:S(2)}) %all-to-all-start) | async-done | bytes 1835040 | tf_op jit(solution)/shard_map/all_to_all | solution.py:52
  60.3 2.0 convolution_convert_fusion.1
  63.9 20.3 %collective-permute-done = bf16[1,4,32,3584]{3,1,2,0:T(4,128)(2,1)S(1)} collective-permute-done((bf16[1,4,32,3584]{3,1,2,0:T(4,128)(2,1)S(1)}, bf16[1,4,32,3584]{3,1,2,0:T(4,128)(2,1)S(1)}, u32[]{:S(2)}, u32[]{:S(2)}) %collective-permute-start) | collective-permute-done | bytes 917536 | tf_op jit(solution)/shard_map/ppermute | solution.py:19
  85.5 2.3 fusion.27
  89.3 2.1 reshape.167
  91.4 2.5 copy.54
  93.9 2.1 reshape.168
  96.0 2.5 copy.55
  99.5 29.2 %collective-permute-done.1 = bf16[2,4,32,3584]{3,1,2,0:T(4,128)(2,1)} collective-permute-done((bf16[2,4,32,3584]{3,1,2,0:T(4,128)(2,1)}, bf16[2,4,32,3584]{3,1,2,0:T(4,128)(2,1)}, u32[]{:S(2)}, u32[]{:S(2)}) %collective-permute-start.1) | collective-permute-done | bytes 1835040 | tf_op jit(solution)/shard_map/ppermute | solution.py:19
  128.7 4.2 pad_maximum_fusion
  134.4 2.6 copy.88
  136.9 8.3 %reshape_reshape.3 = bf16[4,128,4,7,128]{4,3,2,1,0:T(8,128)(2,1)} reshape(bf16[4,4,32,3584]{3,2,1,0:T(8,128)(2,1)} %bitcast.134) | data formatting | bytes 7340032 | tf_op jit(solution)/shard_map/reshape;reshape | solution.py:80
  145.2 5.6 %copy.56 = bf16[4,128,4,7,128]{4,1,3,2,0:T(8,128)(2,1)} copy(bf16[4,128,4,7,128]{4,3,2,1,0:T(8,128)(2,1)} %reshape_reshape.3) | data formatting | bytes 7340032
  150.8 217.7 %while.18 = (s32[]{:T(128)}, f32[16,128,7,128]{1,3,2,0:T(8,128)}, f32[16,128,7]{1,2,0:T(8,128)S(1)}, f32[16,128,7]{1,2,0:T(8,128)S(1)}, s32[16]{0:T(128)S(1)}, /...) while((s32[]{:T(128)}, f32[16,128,7,128]{1,3,2,0:T(8,128)}, ...), condition=%wide.region_8.9_spmd.clone, body=%wide.region_4.8_spmd.clone.sunk | while | flops 483658688 | bytes 12791268 | solution.py:124
  161.4 3.1 fusion.49
  175.0 3.1 fusion.49
  185.0 1.8 fusion.47
  188.6 3.1 fusion.49
  202.2 3.1 fusion.49
  215.8 3.1 fusion.49
  225.8 1.8 fusion.47
  229.4 3.1 fusion.49
  243.0 3.1 fusion.49
  253.0 1.8 fusion.47
  256.6 3.0 fusion.49
  266.6 1.8 fusion.47
  270.2 3.1 fusion.49
  280.2 1.8 fusion.47
  283.8 3.1 fusion.49
  293.8 1.8 fusion.47
  297.4 3.0 fusion.49
  307.4 1.8 fusion.47
  311.0 3.1 fusion.49
  321.0 1.8 fusion.47
  324.6 3.1 fusion.49
  334.7 1.8 fusion.47
  338.3 3.0 fusion.49
  348.3 1.8 fusion.47
  351.9 3.1 fusion.49
  365.5 3.1 fusion.49
  368.6 16.3 %pmax.7 = bf16[4,4,128,7]{2,0,3,1:T(4,128)(2,1)S(1)} all-reduce(bf16[4,4,128,7]{2,0,3,1:T(4,128)(2,1)S(1)} %copy.86), channel_id=1, replica_groups=mesh['replica'=8,'ctx'=4] {'ctx'}, use_global_device_ids=true, to_apply=%region_9.10 | all-reduce | flops 14336 | bytes 57344 | tf_op jit(solution)/shard_map/pmax | solution.py:130
  386.6 2.3 reshape.169
  389.0 6.2 %multiply_convert_fusion.6 = bf16[4,4,128,7,128]{2,4,3,1,0:T(8,128)(2,1)} fusion(f32[4,4,128,7,128]{2,4,3,1,0:T(8,128)} %bitcast.16, f32[4,4,128,7]{2,3,1,0:T(8,128)S(1)} %copy.59), kind=kLoop, calls=%fused_computation.39 | loop fusion | flops 3670016 | bytes 11067392 | tf_op jit(solution)/shard_map/convert_element_type | solution.py:140
  395.2 7.3 %copy.60 = bf16[4,128,3584]{2,0,1:T(4,128)(2,1)} copy(bf16[4,128,3584]{1,2,0:T(8,128)(2,1)} %bitcast.135) | data formatting | bytes 7340032 | tf_op jit(solution)/shard_map/convert_element_type | solution.py:140
  404.5 6.8 %reduce-scatter.4.cloned.1.call-done = bf16[32,112]{1,0:T(8,128)(2,1)} async-done(((bf16[128,112]{1,0:T(8,128)(2,1)}), bf16[32,112]{1,0:T(8,128)(2,1)}) %reduce-scatter.4.cloned.1.call-update) | async-done | bytes 7184
  415.2 94.9 %all-reduce.3.cloned.1.call-done = bf16[4,128,3584]{2,0,1:T(4,128)(2,1)} async-done(((bf16[4,128,3584]{2,0,1:T(4,128)(2,1)}), bf16[4,128,3584]{2,0,1:T(4,128)(2,1)}) %all-reduce.3.cloned.1.call-update) | async-done | bytes 3670032
  511.6 2.7 divide_convert_fusion
  (296 shorter events, 113.3 us)
Async XLA Ops:
  6.5 1.2 copy-start
  8.7 8.2 %copy-start.3 = (s32[32]{0:T(128)S(1)}, s32[32]{0:T(128)}, u32[]{:S(2)}) copy-start(s32[32]{0:T(128)} %param.15) | copy-start | bytes 388
  10.5 49.8 %all-to-all-start = ((bf16[8,32,3584]{2,1,0:T(8,128)(2,1)}), bf16[8,32,3584]{2,1,0:T(8,128)(2,1)S(1)}, u32[]{:S(2)}, u32[]{:S(2)}) async-start(bf16[8,32,3584]{2,1,0:T(8,128)(2,1)} %copy.51), calls=%async_computation | async-start | bytes 3670016 | tf_op jit(solution)/shard_map/all_to_all | solution.py:52
  16.9 394.4 %reduce-scatter.4.cloned.1.call-start = ((), (), s32[]{:S(2)}) async-start(), calls=%async_computation.2 | async-start | bytes 40960
  62.3 21.9 %collective-permute-start = (bf16[1,4,32,3584]{3,1,2,0:T(4,128)(2,1)S(1)}, bf16[1,4,32,3584]{3,1,2,0:T(4,128)(2,1)S(1)}, u32[]{:S(2)}, u32[]{:S(2)}) collective-permute-start(bf16[1,4,32,3584]{3,1,2,0:T(4,128)(2,1)S(1)} %bitcast.137), channel_id=1, source_target_pairs={{0,1},{1,0},{2,3},{3,2},{4,5},{5,4},{6,7},{7,6},{8,9},{9,8},{10,11... | collective-permute-start | bytes 2752520 | tf_op jit(solution)/shard_map/ppermute | solution.py:19
  87.8 40.9 %collective-permute-start.1 = (bf16[2,4,32,3584]{3,1,2,0:T(4,128)(2,1)}, bf16[2,4,32,3584]{3,1,2,0:T(4,128)(2,1)}, u32[]{:S(2)}, u32[]{:S(2)}) collective-permute-start(bf16[2,4,32,3584]{3,1,2,0:T(4,128)(2,1)} %get-tuple-element.372), channel_id=1, source_target_pairs={{0,2},{1,3},{2,0},{3,1},{4,6},{5,7},{6,4},{7,5},{8,10},{9,11},{10,... | collective-permute-start | bytes 5505032 | tf_op jit(solution)/shard_map/ppermute | solution.py:19
  91.4 7.2 %copy-start.2 = (s32[28,32,32]{2,1,0:T(8,128)S(1)}, s32[28,32,32]{2,1,0:T(8,128)}, u32[]{:S(2)}) copy-start(s32[28,32,32]{2,1,0:T(8,128)} %param.14) | copy-start | bytes 344068
  388.9 121.2 %all-reduce.3.cloned.1.call-start = ((), (), s32[]{:S(2)}) async-start(), calls=%async_computation.3 | async-start | bytes 7340032
  402.5 0.7 copy-start.4
  413.6 100.7 %copy-start.1 = (bf16[4,32,3584]{2,1,0:T(8,128)(2,1)S(1)}, bf16[4,32,3584]{2,1,0:T(8,128)(2,1)}, u32[]{:S(2)}) copy-start(bf16[4,32,3584]{2,1,0:T(8,128)(2,1)} %param.9) | copy-start | bytes 2752516
Sparse Core Ops, SparseCore 0:
  389.0 22.1 reduce-scatter.3
  414.4 95.6 all-reduce.2
